TPU v7x, 32 devices: a whole 2x2x4 slice. The times are simulated.
32 devices in a mesh: parts: 2 (over y), samp: 16 (over z, x, core).
Axes of the slice: x: 2, y: 2, z: 4, core: 2. Of those that a mesh axis runs over, the one named last changes fastest.
Arguments:
- expression: bfloat16 [1024, 20480], P(('parts', 'samp')), parts along dimension 0, may hold values from -6 to 6
- current: bfloat16 [1024, 256], P(('parts', 'samp')), parts along dimension 0, may hold values from -6 to 6
- next_packed: int32 [512, 32], P(('parts', 'samp')), parts along dimension 0, may hold values from -2147483648 to 1789569706, as said below
- covariates: float32 [1024, 64], P(('parts', 'samp')), parts along dimension 0, may hold values from -1 to 1
Outputs:
- scores: float32 [40960, 256], P(('parts', 'samp')), parts along dimension 0
- next_block: bfloat16 [1024, 256], P(('parts', 'samp')), parts along dimension 0
There are 2 independent parts, one for each index of `parts`. A program takes and returns all parts, laid end to end along the dimension named above; each array names one. Nothing has to cross between parts.
Inputs may be any that keep to these rules, and one draw needn't show every extreme that they name: Each word holds the dosages (0, 1 or 2) of 16 consecutive samples of one variant, two bits a sample: sample 16 w + j of variant v in bits 2 j and 2 j + 1 of next_packed[v, w], bit 31 being the sign bit of the int32 word.
All inputs are finite; a program needn't handle non-finite values.
Results may differ from a plain program's by a relative error of at most 0.0004.
Values may be sent and summed in bfloat16 or wider, within the bound.
A program may use at most 64 MiB of HBM per device.

v0:
```python
import jax
import jax.numpy as jnp
from jax import lax
from jax.sharding import PartitionSpec as P


def unpack_words(packed_words):
    shifts = 2 * jnp.arange(16, dtype=jnp.int32)
    fields = jnp.bitwise_and(
        lax.shift_right_logical(packed_words[:, :, None], shifts[None, None, :]), 3
    )
    return fields.reshape(packed_words.shape[0], -1).T.astype(jnp.float32)


def over_samples(left, right):
    return lax.dot_general(
        left, right, (((0,), (0,)), ((), ())), preferred_element_type=jnp.float32
    )


def precise_samples(left, right):
    return lax.dot_general(left, right, (((0,), (0,)), ((), ())), precision=lax.Precision.HIGHEST)


def shards(expression, current, next_packed, covariates):
    group_size = lax.axis_size("samp")
    samples_all = expression.shape[0] * group_size
    scale_factor = float(samples_all) ** (-0.5)
    regrouped = lax.all_to_all(expression, "samp", split_axis=1, concat_axis=0, tiled=True)
    scores = (
        over_samples(regrouped, lax.all_gather(current, "samp", axis=0, tiled=True)) * scale_factor
    )
    packed_words = lax.all_to_all(next_packed, "samp", split_axis=1, concat_axis=0, tiled=True)
    dosage = unpack_words(packed_words)
    local_totals = jnp.sum(dosage, axis=0)
    local_proj = precise_samples(covariates, dosage)
    local_covsum = jnp.sum(covariates, axis=0)
    local_squares = jnp.sum(dosage * dosage, axis=0)
    local_gram = precise_samples(covariates, covariates)
    totals, projected, cov_sums, squares, cov_gram = lax.psum(
        (local_totals, local_proj, local_covsum, local_squares, local_gram), "samp"
    )
    average = totals / samples_all
    loading = projected - cov_sums[:, None] * average[None, :]
    leftover = (
        dosage - average[None, :] - jnp.dot(covariates, loading, precision=lax.Precision.HIGHEST)
    )
    mapped = jnp.dot(cov_gram, loading, precision=lax.Precision.HIGHEST)
    sq_norm = (
        squares
        - samples_all * average * average
        - 2.0 * jnp.sum(loading * loading, axis=0)
        + jnp.sum(loading * mapped, axis=0)
    )
    next_block = (leftover * lax.rsqrt(sq_norm / samples_all + 1e-05)[None, :]).astype(jnp.bfloat16)
    return (scores, next_block)


def solution(mesh):
    in_specs = (
        P(("parts", "samp"), None),
        P(("parts", "samp"), None),
        P(("parts", "samp"), None),
        P(("parts", "samp"), None),
    )
    out_specs = (P(("parts", "samp"), None), P(("parts", "samp"), None))
    return jax.shard_map(shards, mesh=mesh, in_specs=in_specs, out_specs=out_specs, check_vma=False)
```

profile of v0, /device:TPU:8, one launch (start us, length us, event | category | flops | bytes accessed | tf_op | source)
XLA Modules:
  0.0 168.2 jit_solution(882091936499760265)
XLA Ops:
  7.2 1.4 copy.12
  8.5 6.3 %all-to-all-start.1 = ((s32[16,16,2]{0,2,1:T(2,128)}), s32[16,16,2]{0,2,1:T(2,128)S(1)}, u32[]{:S(2)}, u32[]{:S(2)}) async-start(s32[16,16,2]{0,2,1:T(2,128)} %bitcast.2), calls=%async_computation.1 | async-start | bytes 32768 | tf_op jit(solution)/shard_map/all_to_all | solution.py:33
  14.8 2.5 %copy.16 = bf16[4,16,8,1280]{3,2,0,1:T(8,128)(2,1)} copy(bf16[4,16,8,1280]{3,2,1,0:T(8,128)(2,1)} %bitcast.37) | data formatting | bytes 2621440 | tf_op jit(solution)/shard_map/all_to_all | solution.py:29
  17.3 2.5 %all-to-all-done.1 = s32[16,16,2]{0,2,1:T(2,128)S(1)} async-done(((s32[16,16,2]{0,2,1:T(2,128)}), s32[16,16,2]{0,2,1:T(2,128)S(1)}, u32[]{:S(2)}, u32[]{:S(2)}) %all-to-all-start.1) | async-done | bytes 2080 | tf_op jit(solution)/shard_map/all_to_all | solution.py:33
  19.8 0.0 copy-start
  19.8 0.0 copy-start.1
  19.8 5.2 %all-to-all-start = ((bf16[32,16,1280]{2,0,1:T(8,128)(2,1)}), bf16[32,16,1280]{2,0,1:T(8,128)(2,1)S(1)}, u32[]{:S(2)}, u32[]{:S(2)}) async-start(bf16[32,16,1280]{2,0,1:T(8,128)(2,1)} %bitcast.36), calls=%async_computation | async-start | bytes 2621440 | tf_op jit(solution)/shard_map/all_to_all | solution.py:29
  25.1 0.0 all-reduce.3.cloned.1.call-start
  25.1 0.1 shift_right_logical.26
  25.2 0.0 copy-done
  25.2 0.0 copy-done.1
  25.2 41.4 %all_gather.3 = bf16[512,256]{1,0:T(8,128)(2,1)S(1)} all-gather(bf16[32,256]{1,0:T(8,128)(2,1)S(1)} %copy-done.1), channel_id=1, replica_groups=mesh['parts'=2,'samp'=16] {'samp'}, dimensions={0}, use_global_device_ids=true | all-gather | bytes 278528 | tf_op jit(solution)/shard_map/all_gather | solution.py:31
  66.6 0.2 fusion.14
  66.9 0.1 shift_right_logical.22
  67.0 0.1 fusion.9
  67.1 0.1 fusion.5
  67.1 0.9 convolution_bitcast_fusion
  68.0 0.0 all-reduce.3.cloned.1.call-update
  68.1 51.9 %all-reduce = (f32[256]{0:T(256)S(1)}, f32[64]{0:T(128)S(1)}, f32[64,64]{1,0:T(8,128)S(1)}, f32[256]{0:T(256)S(1)}) all-reduce(f32[256]{0:T(256)S(1)} %get-tuple-element.3, f32[64]{0:T(128)S(1)} %reduce_sum.46, f32[64,64]{1,0:T(8,128)S(1)} %fusion.14, f32[256]{0:T(256)S(1)} %get-tuple-element.2), channel_id=1, replica_groups=mesh['parts'=2,'samp'=16] {'samp'}, use_global_device_ids=true, to_apply=%region_1.0 | all-reduce | flops 4672 | bytes 37376 | tf_op jit(solution)/shard_map/psum | solution.py:40
  120.0 0.1 fusion.7
  120.0 35.9 %all-reduce.3.cloned.1.call-done = f32[64,256]{1,0:T(8,128)} async-done(((f32[64,256]{1,0:T(8,128)}), f32[64,256]{1,0:T(8,128)}) %all-reduce.3.cloned.1.call-update) | async-done | bytes 65552 | tf_op jit(solution)/shard_map/psum | solution.py:40
  156.0 0.9 multiply_reduce_fusion
  156.9 1.1 fusion
  158.0 1.7 %fusion.3 = bf16[32,256]{1,0:T(8,128)(2,1)} fusion(f32[256,32]{0,1:T(8,128)S(1)} %fusion.7, f32[32,64]{1,0:T(8,128)S(1)} %copy-done, f32[64,256]{1,0:T(8,128)} %all-reduce.3.cloned.1.call-done, f32[256]{0:T(256)S(1)} %broadcast_multiply_fusion, f32[64]{0:T(128)S(1)} %get-tuple-element.5, f32[256]{0:T(256)S(1)} %add_rsqrt_fusion), kind=kOutput, calls=%fused_computation.8 | convolution fusion | flops 6348800 | bytes 125184 | tf_op jit(solution)/shard_map/dot_general | solution.py:46
  159.7 0.0 all-to-all-done
  159.7 1.6 convolution_multiply_fusion
  (6 shorter events, 0.0 us)
Async XLA Ops:
  8.5 11.3 %all-to-all-start.1 = ((s32[16,16,2]{0,2,1:T(2,128)}), s32[16,16,2]{0,2,1:T(2,128)S(1)}, u32[]{:S(2)}, u32[]{:S(2)}) async-start(s32[16,16,2]{0,2,1:T(2,128)} %bitcast.2), calls=%async_computation.1 | async-start | bytes 32768 | tf_op jit(solution)/shard_map/all_to_all | solution.py:33
  19.8 5.4 %copy-start = (f32[32,64]{1,0:T(8,128)S(1)}, f32[32,64]{1,0:T(8,128)}, u32[]{:S(2)}) copy-start(f32[32,64]{1,0:T(8,128)} %param.7) | copy-start | bytes 24580
  19.8 5.4 %copy-start.1 = (bf16[32,256]{1,0:T(8,128)(2,1)S(1)}, bf16[32,256]{1,0:T(8,128)(2,1)}, u32[]{:S(2)}) copy-start(bf16[32,256]{1,0:T(8,128)(2,1)} %param.5) | copy-start | bytes 49156
  19.8 139.9 %all-to-all-start = ((bf16[32,16,1280]{2,0,1:T(8,128)(2,1)}), bf16[32,16,1280]{2,0,1:T(8,128)(2,1)S(1)}, u32[]{:S(2)}, u32[]{:S(2)}) async-start(bf16[32,16,1280]{2,0,1:T(8,128)(2,1)} %bitcast.36), calls=%async_computation | async-start | bytes 2621440 | tf_op jit(solution)/shard_map/all_to_all | solution.py:29
  25.1 130.9 %all-reduce.3.cloned.1.call-start = ((), (), s32[]{:S(2)}) async-start(), calls=%async_computation.2 | async-start | bytes 131072 | tf_op jit(solution)/shard_map/psum | solution.py:40
Sparse Core Ops, SparseCore 0:
  68.2 87.7 all-reduce.2
where the time goes:
time: 169 us; the launch traced here: 168 us
  blocking collectives  93.3 us (55%)
  waiting for transfers between devices  38.5 us (23%)
  between operations  14.1 us (8%)
  starting transfers between devices  11.5 us (7%)
  matrix products  5.53 us (3%)
  local copies, waits for them, and re-layouts  4.06 us (2%)
    psum x1, blocking collectives, shards(): lax.psum((local_totals, local_proj, local_covsum, local_squares, local_gr...  51.9 us
    all_gather x1, blocking collectives, shards(): lax.all_gather(current, 'samp', axis=0, tiled=True)  41.4 us
    psum x1, waiting for transfers between devices, shards(): lax.psum((local_totals, local_proj, local_covsum, local_squares, local_gr...  35.9 us
    all_to_all x1, starting transfers between devices, shards(): lax.all_to_all(next_packed, 'samp', split_axis=1, concat_axis=0, tiled=True)  6.27 us
    all_to_all x1, starting transfers between devices, shards(): lax.all_to_all(expression, 'samp', split_axis=1, concat_axis=0, tiled=True)  5.22 us
  transfers between devices with their start and end apart: 3, of which 2 were waited for; matrix products, arithmetic and copies ran while one was open for 5% of the time, Pallas kernels for 0%

commit v1 on v0

--- a/solution.py
+++ b/solution.py
@@ -30,7 +30,15 @@
     scores = (
         over_samples(regrouped, lax.all_gather(current, "samp", axis=0, tiled=True)) * scale_factor
     )
-    packed_words = lax.all_to_all(next_packed, "samp", split_axis=1, concat_axis=0, tiled=True)
+    packed_words = jnp.concatenate(
+        lax.all_to_all(
+            jnp.stack(jnp.split(next_packed, lax.axis_size("samp"), axis=1), axis=0),
+            axis_name="samp",
+            split_axis=0,
+            concat_axis=0,
+        ),
+        axis=0,
+    )
     dosage = unpack_words(packed_words)
     local_totals = jnp.sum(dosage, axis=0)
     local_proj = precise_samples(covariates, dosage)

time: 169 us -> 179 us (1.059)
  local copies, waits for them, and re-layouts: 4.06 us -> 14.3 us
    unnamed x5 -> x19, local copies, waits for them, and re-layouts: 1.38 us -> 8.48 us
    split x0 -> x17, local copies, waits for them, and re-layouts: none -> 2.64 us  [shards(): jnp.split(next_packed, lax.axis_size('samp'), axis=1)]
  transfers between devices with their start and end apart: 3 -> 3, of which waited for: 2 -> 2; matrix products, arithmetic and copies ran while one was open for 5% -> 4% of each run, Pallas kernels for 0% -> 0%
where the time goes in v1:
time: 179 us
  blocking collectives  93.3 us (52%)
  waiting for transfers between devices  38.5 us (22%)
  local copies, waits for them, and re-layouts  14.3 us (8%)
  between operations  14.1 us (8%)
  starting transfers between devices  11.5 us (6%)
  matrix products  5.53 us (3%)
    psum x1, blocking collectives, shards(): lax.psum((local_totals, local_proj, local_covsum, local_squares, local_gr...  51.9 us
    all_gather x1, blocking collectives, shards(): lax.all_gather(current, 'samp', axis=0, tiled=True)  41.4 us
    psum x1, waiting for transfers between devices, shards(): lax.psum((local_totals, local_proj, local_covsum, local_squares, local_gr...  35.9 us
    unnamed x19, local copies, waits for them, and re-layouts  8.48 us
    all_to_all x1, starting transfers between devices, shards(): lax.all_to_all(jnp.stack(jnp.split(next_packed, lax.axis_size('samp'), ax...  6.27 us
    all_to_all x1, starting transfers between devices, shards(): lax.all_to_all(expression, 'samp', split_axis=1, concat_axis=0, tiled=True)  5.22 us
  transfers between devices with their start and end apart: 3, of which 2 were waited for; matrix products, arithmetic and copies ran while one was open for 4% of the time, Pallas kernels for 0%

profile of v1, /device:TPU:8, one launch (start us, length us, event | category | flops | bytes accessed | tf_op | source)
XLA Modules:
  0.0 178.5 jit_solution(13629580522161657270)
XLA Ops:
  7.2 1.4 fusion.14
  8.5 0.1 copy.58
  8.6 0.6 constant_dynamic-update-slice_fusion.15
  9.2 0.1 copy.59
  9.3 0.1 copy.60
  9.4 0.1 copy.61
  9.4 0.1 copy.62
  9.5 0.1 copy.63
  9.6 0.1 copy.64
  9.7 0.1 copy.65
  9.8 0.1 copy.66
  9.8 0.1 copy.67
  9.9 0.1 copy.68
  10.0 0.1 copy.69
  10.1 0.1 copy.70
  10.1 0.1 copy.71
  10.2 0.1 copy.72
  10.3 0.1 copy.73
  10.4 0.6 constant_dynamic-update-slice_fusion.14
  11.0 0.6 constant_dynamic-update-slice_fusion.13
  11.5 0.6 constant_dynamic-update-slice_fusion.12
  12.1 0.6 constant_dynamic-update-slice_fusion.11
  12.7 0.6 constant_dynamic-update-slice_fusion.10
  13.2 0.6 constant_dynamic-update-slice_fusion.9
  13.8 0.6 constant_dynamic-update-slice_fusion.8
  14.4 0.6 constant_dynamic-update-slice_fusion.7
  14.9 0.6 constant_dynamic-update-slice_fusion.6
  15.5 0.6 constant_dynamic-update-slice_fusion.5
  16.0 0.6 constant_dynamic-update-slice_fusion.4
  16.6 0.6 constant_dynamic-update-slice_fusion.3
  17.2 0.6 constant_dynamic-update-slice_fusion.2
  17.7 0.6 constant_dynamic-update-slice_fusion.1
  18.3 0.6 constant_dynamic-update-slice_fusion
  18.9 6.3 %all-to-all-start.1 = ((s32[16,16,2]{1,2,0:T(2,128)}), s32[16,16,2]{1,2,0:T(2,128)S(1)}, u32[]{:S(2)}, u32[]{:S(2)}) async-start(s32[16,16,2]{1,2,0:T(2,128)} %constant_dynamic-update-slice_fusion), calls=%async_computation.1 | async-start | bytes 32768 | tf_op jit(solution)/shard_map/all_to_all | solution.py:34
  25.1 2.5 %copy.77 = bf16[4,16,8,1280]{3,2,0,1:T(8,128)(2,1)} copy(bf16[4,16,8,1280]{3,2,1,0:T(8,128)(2,1)} %bitcast.67) | data formatting | bytes 2621440 | tf_op jit(solution)/shard_map/all_to_all | solution.py:29
  27.6 2.5 %all-to-all-done.1 = s32[16,16,2]{1,2,0:T(2,128)S(1)} async-done(((s32[16,16,2]{1,2,0:T(2,128)}), s32[16,16,2]{1,2,0:T(2,128)S(1)}, u32[]{:S(2)}, u32[]{:S(2)}) %all-to-all-start.1) | async-done | bytes 2080 | tf_op jit(solution)/shard_map/all_to_all | solution.py:34
  30.2 0.0 copy-start
  30.2 0.0 copy-start.1
  30.2 5.2 %all-to-all-start = ((bf16[32,16,1280]{2,0,1:T(8,128)(2,1)}), bf16[32,16,1280]{2,0,1:T(8,128)(2,1)S(1)}, u32[]{:S(2)}, u32[]{:S(2)}) async-start(bf16[32,16,1280]{2,0,1:T(8,128)(2,1)} %bitcast.66), calls=%async_computation | async-start | bytes 2621440 | tf_op jit(solution)/shard_map/all_to_all | solution.py:29
  35.4 0.0 all-reduce.3.cloned.1.call-start
  35.4 0.1 shift_right_logical.26
  35.5 0.0 copy-done
  35.5 0.0 copy-done.1
  35.5 41.4 %all_gather.3 = bf16[512,256]{1,0:T(8,128)(2,1)S(1)} all-gather(bf16[32,256]{1,0:T(8,128)(2,1)S(1)} %copy-done.1), channel_id=1, replica_groups=mesh['parts'=2,'samp'=16] {'samp'}, dimensions={0}, use_global_device_ids=true | all-gather | bytes 278528 | tf_op jit(solution)/shard_map/all_gather | solution.py:31
  77.0 0.2 fusion.15
  77.2 0.1 shift_right_logical.22
  77.3 0.1 fusion.9
  77.4 0.1 fusion.5
  77.5 0.9 convolution_bitcast_fusion
  78.3 0.0 all-reduce.3.cloned.1.call-update
  78.4 51.9 %all-reduce = (f32[256]{0:T(256)S(1)}, f32[64]{0:T(128)S(1)}, f32[64,64]{1,0:T(8,128)S(1)}, f32[256]{0:T(256)S(1)}) all-reduce(f32[256]{0:T(256)S(1)} %get-tuple-element.3, f32[64]{0:T(128)S(1)} %reduce_sum.46, f32[64,64]{1,0:T(8,128)S(1)} %fusion.15, f32[256]{0:T(256)S(1)} %get-tuple-element.2), channel_id=1, replica_groups=mesh['parts'=2,'samp'=16] {'samp'}, use_global_device_ids=true, to_apply=%region_1.0 | all-reduce | flops 4672 | bytes 37376 | tf_op jit(solution)/shard_map/psum | solution.py:48
  130.3 0.1 fusion.7
  130.4 35.9 %all-reduce.3.cloned.1.call-done = f32[64,256]{1,0:T(8,128)} async-done(((f32[64,256]{1,0:T(8,128)}), f32[64,256]{1,0:T(8,128)}) %all-reduce.3.cloned.1.call-update) | async-done | bytes 65552 | tf_op jit(solution)/shard_map/psum | solution.py:48
  166.3 0.9 multiply_reduce_fusion
  167.2 1.1 fusion
  168.4 1.7 fusion.3
  170.1 0.0 all-to-all-done
  170.1 1.6 convolution_multiply_fusion
  (6 shorter events, 0.0 us)
Async XLA Ops:
  18.9 11.3 %all-to-all-start.1 = ((s32[16,16,2]{1,2,0:T(2,128)}), s32[16,16,2]{1,2,0:T(2,128)S(1)}, u32[]{:S(2)}, u32[]{:S(2)}) async-start(s32[16,16,2]{1,2,0:T(2,128)} %constant_dynamic-update-slice_fusion), calls=%async_computation.1 | async-start | bytes 32768 | tf_op jit(solution)/shard_map/all_to_all | solution.py:34
  30.2 5.4 %copy-start = (f32[32,64]{1,0:T(8,128)S(1)}, f32[32,64]{1,0:T(8,128)}, u32[]{:S(2)}) copy-start(f32[32,64]{1,0:T(8,128)} %param.7) | copy-start | bytes 24580
  30.2 5.4 %copy-start.1 = (bf16[32,256]{1,0:T(8,128)(2,1)S(1)}, bf16[32,256]{1,0:T(8,128)(2,1)}, u32[]{:S(2)}) copy-start(bf16[32,256]{1,0:T(8,128)(2,1)} %param.5) | copy-start | bytes 49156
  30.2 139.9 %all-to-all-start = ((bf16[32,16,1280]{2,0,1:T(8,128)(2,1)}), bf16[32,16,1280]{2,0,1:T(8,128)(2,1)S(1)}, u32[]{:S(2)}, u32[]{:S(2)}) async-start(bf16[32,16,1280]{2,0,1:T(8,128)(2,1)} %bitcast.66), calls=%async_computation | async-start | bytes 2621440 | tf_op jit(solution)/shard_map/all_to_all | solution.py:29
  35.4 130.9 %all-reduce.3.cloned.1.call-start = ((), (), s32[]{:S(2)}) async-start(), calls=%async_computation.2 | async-start | bytes 131072 | tf_op jit(solution)/shard_map/psum | solution.py:48
Sparse Core Ops, SparseCore 0:
  78.5 87.7 all-reduce.2
